TPU v7x, 32 devices: a whole 2x2x4 slice. The times are simulated.
32 devices in a mesh: seq: 8 (over y, x, core), tensor: 4 (over z).
Axes of the slice: x: 2, y: 2, z: 4, core: 2. Of those that a mesh axis runs over, the one named last changes fastest.
Arguments:
- tokens: bfloat16 [4096, 8192], P('seq', 'tensor'), may hold values from -6 to 6
- positions: int32 [4096], P('seq'), may hold values from 0 to 4095, each once
- norm_gain: float32 [8192], replicated, may hold values from 0.1 to 1.9
- w_query: bfloat16 [8192, 4096], P('seq', 'tensor'), may hold values from -0.0625 to 0.0625
- w_key: bfloat16 [8192, 1024], P('seq', 'tensor'), may hold values from -0.0625 to 0.0625
- w_value: bfloat16 [8192, 1024], P('seq', 'tensor'), may hold values from -0.0625 to 0.0625
- b_query: float32 [4096], P('tensor'), may hold values from -40 to 40
- b_key: float32 [1024], P('tensor'), may hold values from -40 to 40
- b_value: float32 [1024], P('tensor'), may hold values from -6 to 6
- w_out: bfloat16 [4096, 8192], P('tensor', 'seq'), may hold values from -0.09375 to 0.09375
Outputs:
- mixed: bfloat16 [4096, 8192], P('seq', 'tensor')
- context: bfloat16 [4096, 4096], P('seq', 'tensor')
Inputs may be any that keep to these rules, and one draw needn't show every extreme that they name: positions holds every position 0 to 4095 once.
All inputs are finite; a program needn't handle non-finite values.
Results may differ from a plain program's by a relative error of at most 0.025.
Values may be sent and summed in bfloat16 or wider, within the bound.
A program may use at most 128 MiB of HBM per device.

v0:
```python
import math
import jax
import jax.numpy as jnp
from jax import lax
from jax.sharding import PartitionSpec as P

HD = 128
NORM_EPS = 1e-06
ROPE_BASE = 1000000.0
NEG_FILL = -1e30


def rotate(values_in, positions):
    half_dim = HD // 2
    inv_freq = ROPE_BASE ** (-jnp.arange(half_dim, dtype=jnp.float32) * 2.0 / HD)
    angles = positions.astype(jnp.float32)[:, None] * inv_freq[None, :]
    cosine = jnp.cos(angles)[:, None, :]
    sines = jnp.sin(angles)[:, None, :]
    lower_half = values_in[..., :half_dim]
    upper_half = values_in[..., half_dim:]
    return jnp.concatenate(
        [lower_half * cosine - upper_half * sines, upper_half * cosine + lower_half * sines], -1
    )


def shards(tokens, positions, norm_gain, w_query, w_key, w_value, b_query, b_key, b_value, w_out):
    tok_rows = tokens.shape[0]
    features = lax.all_gather(tokens, "tensor", axis=1, tiled=True)
    inputs = features.astype(jnp.float32)
    inverse_rms = lax.rsqrt(jnp.mean(inputs * inputs, -1, keepdims=True) + NORM_EPS)
    normed = (inputs * inverse_rms * norm_gain[None, :]).astype(jnp.bfloat16)
    w_cat = jnp.concatenate((w_query, w_key, w_value), 1)
    b_cat = jnp.concatenate((b_query, b_key, b_value))
    projected = jnp.dot(
        normed, lax.all_gather(w_cat, "seq", axis=0, tiled=True), preferred_element_type=jnp.float32
    )
    projected = projected + b_cat[None, :]
    query_cols = w_query.shape[1]
    key_cols = w_key.shape[1]
    heads_here = query_cols // HD
    kv_here = key_cols // HD
    group = heads_here // kv_here
    queries = rotate(projected[:, :query_cols].reshape(tok_rows, heads_here, HD), positions).astype(
        jnp.bfloat16
    )
    queries = queries.reshape(tok_rows, kv_here, group, HD)
    keys_rot = rotate(
        projected[:, query_cols : query_cols + key_cols].reshape(tok_rows, kv_here, HD), positions
    ).astype(jnp.bfloat16)
    values = (
        projected[:, query_cols + key_cols :].astype(jnp.bfloat16).reshape(tok_rows, kv_here, HD)
    )
    scale = HD ** (-0.5)

    def attend_block(running, key_block):
        running_max, denominator, numerator = running
        block_keys, block_values, key_pos = key_block
        scores = (
            jnp.einsum("tgcd,sgd->gcts", queries, block_keys, preferred_element_type=jnp.float32)
            * scale
        )
        allowed = (key_pos[None, :] <= positions[:, None])[None, None, :, :]
        scores = jnp.where(allowed, scores, NEG_FILL)
        new_max = jnp.maximum(running_max, jnp.max(scores, -1))
        weights = jnp.where(allowed, jnp.exp(scores - new_max[..., None]), 0.0)
        rescale = jnp.exp(running_max - new_max)
        denominator = denominator * rescale + jnp.sum(weights, -1)
        numerator = numerator * rescale[..., None] + jnp.einsum(
            "gcts,sgd->gctd",
            weights.astype(jnp.bfloat16),
            block_values,
            preferred_element_type=jnp.float32,
        )
        return (new_max, denominator, numerator)

    start_state = (
        jnp.full((kv_here, group, tok_rows), NEG_FILL, jnp.float32),
        jnp.zeros((kv_here, group, tok_rows), jnp.float32),
        jnp.zeros((kv_here, group, tok_rows, HD), jnp.float32),
    )
    all_keys_in = lax.all_gather(keys_rot, "seq", axis=0, tiled=True)
    all_values_in = lax.all_gather(values, "seq", axis=0, tiled=True)
    key_pos = lax.all_gather(positions, "seq", axis=0, tiled=True)
    count = all_keys_in.shape[0]
    width = math.gcd(count, 2048)
    stacked = (
        all_keys_in.reshape(count // width, width, kv_here, HD),
        all_values_in.reshape(count // width, width, kv_here, HD),
        key_pos.reshape(count // width, width),
    )

    def stepper(carried, key_block):
        return (attend_block(carried, key_block), None)

    result, unused = lax.scan(stepper, start_state, stacked)
    unused_max, denominator, numerator = result
    per_head = numerator / denominator[..., None]
    context = (
        jnp.transpose(per_head, (2, 0, 1, 3))
        .reshape(tok_rows, heads_here * HD)
        .astype(jnp.bfloat16)
    )
    out_terms = jnp.dot(
        context,
        lax.all_gather(w_out, "seq", axis=1, tiled=True),
        preferred_element_type=jnp.float32,
    )
    summed = lax.psum_scatter(
        out_terms.astype(jnp.bfloat16), "tensor", scatter_dimension=1, tiled=True
    ).astype(jnp.float32)
    mixed = (tokens.astype(jnp.float32) + summed).astype(jnp.bfloat16)
    return (mixed, context)


def solution(mesh):
    in_specs = (
        P("seq", "tensor"),
        P("seq"),
        P(),
        P("seq", "tensor"),
        P("seq", "tensor"),
        P("seq", "tensor"),
        P("tensor"),
        P("tensor"),
        P("tensor"),
        P("tensor", "seq"),
    )
    out_specs = (P("seq", "tensor"), P("seq", "tensor"))
    return jax.shard_map(shards, mesh=mesh, in_specs=in_specs, out_specs=out_specs, check_vma=False)
```

profile of v0, /device:TPU:0, one launch (start us, length us, event | category | flops | bytes accessed | tf_op | source)
XLA Modules:
  0.0 640.7 jit_solution(5669417840117130354)
XLA Ops:
  7.2 0.7 all-gather.7.cloned.1.call-update
  8.0 3.1 pad_maximum_fusion
  11.3 1.8 multiply_cosine_fusion
  13.1 148.9 %all-gather.7.cloned.1.call-done = bf16[512,8192]{1,0:T(8,128)(2,1)} async-done(((bf16[512,2048]{1,0:T(8,128)(2,1)}), bf16[512,8192]{1,0:T(8,128)(2,1)}) %all-gather.7.cloned.1.call-update) | async-done | bytes 8388624 | tf_op jit(solution)/shard_map/all_gather | solution.py:28
  161.9 5.1 fusion.20
  167.0 120.2 %all-gather.9.cloned.1.call-done = bf16[8192,1536]{1,0:T(8,128)(2,1)} async-done(((bf16[1024,1536]{1,0:T(8,128)(2,1)}), bf16[8192,1536]{1,0:T(8,128)(2,1)}) %all-gather.9.cloned.1.call-update) | async-done | bytes 25165840 | tf_op jit(solution)/shard_map/all_gather | solution.py:35
  287.2 19.5 %fusion.27 = f32[512,1536]{1,0:T(8,128)S(1)} fusion(bf16[8192,1536]{1,0:T(8,128)(2,1)} %all-gather.9.cloned.1.call-done, bf16[512,8192]{1,0:T(8,128)(2,1)} %all-gather.7.cloned.1.call-done, f32[8192]{0:T(1024)S(1)} %copy-done.10, f32[512]{0:T(512)S(1)} %add_rsqrt_fusion, f32[1536]{0:T(1024)S(1)} %pad_maximum_fusion.3), kind=kOutput, calls=%fused_computation.35 | convolution fusion | flops 12902465536 | bytes 36741120 | tf_op jit(solution)/shard_map/dot_general | solution.py:34
  306.7 1.6 copy-done.1
  308.7 0.6 fusion.32
  309.3 1.2 subtract_convert_fusion.1
  310.6 0.8 pad_maximum_fusion.2
  311.5 1.8 copy_bitcast_fusion
  313.9 8.9 %all-gather = s32[8,1,512]{2,1,0:T(1,128)S(1)} all-gather(s32[1,1,512]{2,1,0:T(1,128)S(1)} %bitcast.69), channel_id=1, replica_groups=mesh['seq'=8,'tensor'=4] {'seq'}, dimensions={0}, use_global_device_ids=true | all-gather | bytes 18432 | tf_op jit(solution)/shard_map/all_gather | solution.py:83
  323.8 0.8 subtract_convert_fusion
  325.0 1.5 pad_maximum_fusion.1
  326.5 12.8 %all-gather.11.cloned.1.call-done = bf16[4096,2,128]{2,0,1:T(8,128)(2,1)} async-done(((bf16[512,2,128]{2,0,1:T(8,128)(2,1)}), bf16[4096,2,128]{2,0,1:T(8,128)(2,1)}) %all-gather.11.cloned.1.call-update) | async-done | bytes 2097168 | tf_op jit(solution)/shard_map/all_gather | solution.py:81
  339.3 29.6 %all-gather.13.cloned.1.call-done = bf16[4096,2,128]{2,0,1:T(8,128)(2,1)} async-done(((bf16[512,2,128]{2,0,1:T(8,128)(2,1)}), bf16[4096,2,128]{2,0,1:T(8,128)(2,1)}) %all-gather.13.cloned.1.call-update) | async-done | bytes 2097168 | tf_op jit(solution)/shard_map/all_gather | solution.py:82
  368.9 97.0 %while.15 = (s32[]{:T(128)}, f32[2,4,512]{2,1,0:T(4,128)S(1)}, f32[2,4,512]{2,1,0:T(4,128)S(1)}, f32[2,4,512,128]{3,2,1,0:T(8,128)S(1)}, s32[2,2048]{1,0:T(2,128...) while((s32[]{:T(128)}, f32[2,4,512]{2,1,0:T(4,128)S(1)}, ...), condition=%wide.region_4.5_spmd.clone, body=%wide.region_1.4_spmd.clone.sunk | while | flops 4406661120 | bytes 112487544 | solution.py:95
  368.9 0.8 broadcast_compare_fusion.2
  369.7 16.7 %fusion.48 = (f32[2,4,512]{2,1,0:T(4,128)S(1)}, f32[2,2048,512,4]{2,1,3,0:T(8,128)}) fusion(pred[512,2048]{0,1:T(8,128)(4,1)S(1)} %broadcast_compare_fusion.2, bf16[512,2,4,128]{3,0,2,1:T(8,128)(2,1)} %get-tuple-element.222, bf16[2,2048,2,128]{3,1,0,2:T(8,128)(2,1)} %get-tuple-element.221, s32[]{:T(128)} %get-tuple-element.204), kind=kOutput, calls=%fused_computation.2.clone.1 | convolution fusion | flops 2172645376 | bytes 36717056 | tf_op jit(solution)/shard_map/while/body/eval_jaxpr/tgcd,sgd->gcts/dot_general | solution.py:59
  386.4 14.9 %fusion.49 = f32[2,4,512]{2,1,0:T(4,128)S(1)} fusion(f32[2,2048,512,4]{2,1,3,0:T(8,128)} %get-tuple-element.190, f32[2,4,512]{2,1,0:T(4,128)S(1)} %select_maximum_fusion.2, pred[512,2048]{0,1:T(8,128)(4,1)S(1)} %broadcast_compare_fusion.2), kind=kLoop, calls=%fused_computation.4.clone.1 | loop fusion | flops 41938944 | bytes 34635776 | tf_op jit(solution)/shard_map/while/body/eval_jaxpr/reduce_sum | solution.py:67
  401.3 17.8 %fusion.51 = f32[2,4,512,128]{3,2,1,0:T(8,128)S(1)} fusion(f32[2,4,512,128]{3,2,1,0:T(8,128)S(1)} %get-tuple-element.207, f32[2,2048,512,4]{2,1,3,0:T(8,128)} %get-tuple-element.190, f32[2,4,512]{2,1,0:T(4,128)S(1)} %select_maximum_fusion.2, pred[512,2048]{0,1:T(8,128)(4,1)S(1)} %broadcast_compare_fusion.2, ...), kind=kOutput, calls=%fused_computation.8.clone.1 | convolution fusion | flops 2190999552 | bytes 39879168 | tf_op jit(solution)/shard_map/while/body/eval_jaxpr/gcts,sgd->gctd/dot_general | solution.py:68
  419.2 0.8 broadcast_compare_fusion.2
  420.0 15.0 %fusion.48 = (f32[2,4,512]{2,1,0:T(4,128)S(1)}, f32[2,2048,512,4]{2,1,3,0:T(8,128)}) fusion(pred[512,2048]{0,1:T(8,128)(4,1)S(1)} %broadcast_compare_fusion.2, bf16[512,2,4,128]{3,0,2,1:T(8,128)(2,1)} %get-tuple-element.222, bf16[2,2048,2,128]{3,1,0,2:T(8,128)(2,1)} %get-tuple-element.221, s32[]{:T(128)} %get-tuple-element.204), kind=kOutput, calls=%fused_computation.2.clone.1 | convolution fusion | flops 2172645376 | bytes 36717056 | tf_op jit(solution)/shard_map/while/body/eval_jaxpr/tgcd,sgd->gcts/dot_general | solution.py:59
  435.0 15.4 %fusion.49 = f32[2,4,512]{2,1,0:T(4,128)S(1)} fusion(f32[2,2048,512,4]{2,1,3,0:T(8,128)} %get-tuple-element.190, f32[2,4,512]{2,1,0:T(4,128)S(1)} %select_maximum_fusion.2, pred[512,2048]{0,1:T(8,128)(4,1)S(1)} %broadcast_compare_fusion.2), kind=kLoop, calls=%fused_computation.4.clone.1 | loop fusion | flops 41938944 | bytes 34635776 | tf_op jit(solution)/shard_map/while/body/eval_jaxpr/reduce_sum | solution.py:67
  450.4 15.5 %fusion.51 = f32[2,4,512,128]{3,2,1,0:T(8,128)S(1)} fusion(f32[2,4,512,128]{3,2,1,0:T(8,128)S(1)} %get-tuple-element.207, f32[2,2048,512,4]{2,1,3,0:T(8,128)} %get-tuple-element.190, f32[2,4,512]{2,1,0:T(4,128)S(1)} %select_maximum_fusion.2, pred[512,2048]{0,1:T(8,128)(4,1)S(1)} %broadcast_compare_fusion.2, ...), kind=kOutput, calls=%fused_computation.8.clone.1 | convolution fusion | flops 2190999552 | bytes 39879168 | tf_op jit(solution)/shard_map/while/body/eval_jaxpr/gcts,sgd->gctd/dot_general | solution.py:68
  465.9 0.7 fusion.30
  466.6 0.8 copy.33
  467.5 0.8 convert_element_type.44
  468.3 17.2 %convolution_convert_fusion = bf16[512,8192]{1,0:T(8,128)(2,1)} fusion(bf16[512,1024]{1,0:T(8,128)(2,1)S(1)} %convert_element_type.44, bf16[1024,8192]{1,0:T(8,128)(2,1)} %all-gather.15.cloned.1.call-done), kind=kOutput, calls=%fused_computation.30 | convolution fusion | flops 8594128896 | bytes 26214400 | tf_op jit(solution)/shard_map/dot_general | solution.py:103
  485.5 144.7 %reduce-scatter.2.cloned.1.call-done = bf16[512,2048]{1,0:T(8,128)(2,1)} async-done(((bf16[512,8192]{1,0:T(8,128)(2,1)}), bf16[512,2048]{1,0:T(8,128)(2,1)}) %reduce-scatter.2.cloned.1.call-update) | async-done | bytes 2097168 | tf_op jit(solution)/shard_map/reduce_scatter | solution.py:108
  630.2 3.7 add_convert_fusion
  (56 shorter events, 2.6 us)
Async XLA Ops:
  7.2 154.7 %all-gather.7.cloned.1.call-start = ((), (), s32[]{:S(2)}) async-start(), calls=%async_computation.1 | async-start | bytes 10485760 | tf_op jit(solution)/shard_map/all_gather | solution.py:28
  7.9 3.3 copy-start.6
  7.9 3.3 copy-start.7
  7.9 3.3 copy-start.8
  7.9 3.3 copy-start.9
  7.9 279.3 %all-gather.9.cloned.1.call-start = ((), (), s32[]{:S(2)}) async-start(), calls=%async_computation.2 | async-start | bytes 28311552 | tf_op jit(solution)/shard_map/all_gather | solution.py:35
  11.2 328.2 %all-gather.11.cloned.1.call-start = ((), (), s32[]{:S(2)}) async-start(), calls=%async_computation.3 | async-start | bytes 2359296 | tf_op jit(solution)/shard_map/all_gather | solution.py:81
  13.1 274.2 %copy-start.10 = (f32[8192]{0:T(1024)S(1)}, f32[8192]{0:T(1024)}, u32[]{:S(2)}) copy-start(f32[8192]{0:T(1024)} %param.14) | copy-start | bytes 98308
  306.7 1.7 copy-start.1
  309.3 13.6 %copy-start.2 = (f32[512,1536]{1,0:T(8,128)S(1)}, f32[512,1536]{1,0:T(8,128)}, u32[]{:S(2)}) copy-start(f32[512,1536]{1,0:T(8,128)} %copy-done.1) | copy-start | bytes 9437188
  311.4 57.5 %all-gather.13.cloned.1.call-start = ((), (), s32[]{:S(2)}) async-start(), calls=%async_computation.4 | async-start | bytes 2359296 | tf_op jit(solution)/shard_map/all_gather | solution.py:82
  313.3 155.0 %all-gather.15.cloned.1.call-start = ((), (), s32[]{:S(2)}) async-start(), calls=%async_computation.5 | async-start | bytes 18874368 | tf_op jit(solution)/shard_map/all_gather | solution.py:105
  313.9 316.3 %reduce-scatter.2.cloned.1.call-start = ((), (), s32[]{:S(2)}) async-start(), calls=%async_computation.6 | async-start | bytes 10485760 | tf_op jit(solution)/shard_map/reduce_scatter | solution.py:108
  322.9 1.0 copy-start.3
  324.7 44.3 %copy-start.4 = (f32[2,4,512,128]{3,2,1,0:T(8,128)S(1)}, f32[2,4,512,128]{3,2,1,0:T(8,128)}, u32[]{:S(2)}) copy-start(f32[2,4,512,128]{3,2,1,0:T(8,128)} %custom-call.2) | copy-start | bytes 6291460
  468.2 17.2 %copy-start.5 = (bf16[512,1024]{1,0:T(8,128)(2,1)}, bf16[512,1024]{1,0:T(8,128)(2,1)S(1)}, u32[]{:S(2)}) copy-start(bf16[512,1024]{1,0:T(8,128)(2,1)S(1)} %convert_element_type.44) | copy-start | bytes 3145732
  485.4 144.7 %copy-start = (bf16[512,2048]{1,0:T(8,128)(2,1)S(1)}, bf16[512,2048]{1,0:T(8,128)(2,1)}, u32[]{:S(2)}) copy-start(bf16[512,2048]{1,0:T(8,128)(2,1)} %param.12) | copy-start | bytes 6291460
Sparse Core Ops, SparseCore 0:
  9.5 152.3 all-gather.6
  163.8 123.3 all-gather.8
  311.5 27.7 all-gather.10
  341.1 27.7 all-gather.12
  370.7 89.7 all-gather.14
  485.6 144.5 reduce-scatter.1
where the time goes:
time: 641 us
  waiting for transfers between devices  457 us (71%)
  matrix products  102 us (16%)
  other arithmetic  50.8 us (8%)
  between operations  14.4 us (2%)
  blocking collectives  8.87 us (1%)
  local copies, waits for them, and re-layouts  7.19 us (1%)
    all_gather x1, waiting for transfers between devices, shards(): features = lax.all_gather(tokens, 'tensor', axis=1, tiled=True)  149 us
    reduce_scatter x1, waiting for transfers between devices, shards(): lax.psum_scatter(out_terms.astype(jnp.bfloat16), 'tensor', scatter_dimens...  145 us
    all_gather x1, waiting for transfers between devices, shards(): lax.all_gather(w_cat, 'seq', axis=0, tiled=True)  120 us
    dot_general x2, matrix products, attend_block(): jnp.einsum('gcts,sgd->gctd', weights.astype(jnp.bfloat16), block_values,...  33.3 us
    dot_general x2, matrix products, attend_block(): jnp.einsum('tgcd,sgd->gcts', queries, block_keys, preferred_element_type=...  31.7 us
    reduce_sum x2, other arithmetic, attend_block(): denominator = denominator * rescale + jnp.sum(weights, -1)  30.2 us
    all_gather x1, waiting for transfers between devices, shards(): all_values_in = lax.all_gather(values, 'seq', axis=0, tiled=True)  29.6 us
    dot_general x1, matrix products, shards(): jnp.dot(normed, lax.all_gather(w_cat, 'seq', axis=0, tiled=True), preferr...  19.5 us
  transfers between devices with their start and end apart: 6, of which 5 were waited for; matrix products, arithmetic and copies ran while one was open for 18% of the time, Pallas kernels for 0%

commit v1 on v0

--- a/solution.py
+++ b/solution.py
@@ -25,7 +25,14 @@
 
 def shards(tokens, positions, norm_gain, w_query, w_key, w_value, b_query, b_key, b_value, w_out):
     tok_rows = tokens.shape[0]
-    features = lax.all_gather(tokens, "tensor", axis=1, tiled=True)
+    ring = [tokens]
+    for hop in range(3):
+        ring.append(lax.ppermute(ring[-1], "tensor", [(dev, (dev + 1) % 4) for dev in range(4)]))
+    features = jnp.roll(
+        jnp.concatenate(ring[::-1], axis=1),
+        (lax.axis_index("tensor") + 1) * ring[0].shape[1],
+        axis=1,
+    )
     inputs = features.astype(jnp.float32)
     inverse_rms = lax.rsqrt(jnp.mean(inputs * inputs, -1, keepdims=True) + NORM_EPS)
     normed = (inputs * inverse_rms * norm_gain[None, :]).astype(jnp.bfloat16)

time: 641 us -> 526 us (0.82)
  waiting for transfers between devices: 457 us -> 328 us
  local copies, waits for them, and re-layouts: 7.19 us -> 23.4 us
    all_gather x1 -> x0, waiting for transfers between devices: 149 us -> none  [shards(): features = lax.all_gather(tokens, 'tensor', axis=1, tiled=True)]
    ppermute x0 -> x3, waiting for transfers between devices: none -> 143 us  [shards(): lax.ppermute(ring[-1], 'tensor', [(dev, (dev + 1) % 4) for dev in range(4)])]
    all_gather x1, waiting for transfers between devices: 120 us -> 0.02 us  [shards(): lax.all_gather(w_cat, 'seq', axis=0, tiled=True)]
    unnamed x24 -> x33, local copies, waits for them, and re-layouts: 2.62 us -> 18.6 us
  transfers between devices with their start and end apart: 6 -> 8, of which waited for: 5 -> 6; matrix products, arithmetic and copies ran while one was open for 18% -> 22% of each run, Pallas kernels for 0% -> 0%
where the time goes in v1:
time: 526 us; the launch traced here: 525 us
  waiting for transfers between devices  328 us (62%)
  matrix products  102 us (19%)
  other arithmetic  45.7 us (9%)
  local copies, waits for them, and re-layouts  23.4 us (4%)
  between operations  14.1 us (3%)
  blocking collectives  8.84 us (2%)
    reduce_scatter x1, waiting for transfers between devices, shards(): lax.psum_scatter(out_terms.astype(jnp.bfloat16), 'tensor', scatter_dimens...  145 us
    ppermute x3, waiting for transfers between devices, shards(): lax.ppermute(ring[-1], 'tensor', [(dev, (dev + 1) % 4) for dev in range(4)])  143 us
    dot_general x2, matrix products, attend_block(): jnp.einsum('gcts,sgd->gctd', weights.astype(jnp.bfloat16), block_values,...  33.3 us
    dot_general x2, matrix products, attend_block(): jnp.einsum('tgcd,sgd->gcts', queries, block_keys, preferred_element_type=...  31.7 us
    reduce_sum x2, other arithmetic, attend_block(): denominator = denominator * rescale + jnp.sum(weights, -1)  30.2 us
    all_gather x1, waiting for transfers between devices, shards(): all_values_in = lax.all_gather(values, 'seq', axis=0, tiled=True)  29.7 us
    dot_general x1, matrix products, shards(): jnp.dot(normed, lax.all_gather(w_cat, 'seq', axis=0, tiled=True), preferr...  19.5 us
    unnamed x33, local copies, waits for them, and re-layouts  18.6 us
  transfers between devices with their start and end apart: 8, of which 6 were waited for; matrix products, arithmetic and copies ran while one was open for 22% of the time, Pallas kernels for 0%

profile of v1, /device:TPU:0, one launch (start us, length us, event | category | flops | bytes accessed | tf_op | source)
XLA Modules:
  0.0 524.9 jit_solution(16105082663449308208)
XLA Ops:
  7.3 3.3 pad_maximum_fusion
  10.6 3.1 collective-permute-start
  13.8 47.7 %collective-permute-done = bf16[512,2048]{1,0:T(8,128)(2,1)S(1)} collective-permute-done((bf16[512,2048]{1,0:T(8,128)(2,1)S(1)}, bf16[512,2048]{1,0:T(8,128)(2,1)S(1)}, u32[]{:S(2)}, u32[]{:S(2)}) %collective-permute-start) | collective-permute-done | bytes 2097184 | tf_op jit(solution)/shard_map/ppermute | solution.py:30
  61.4 1.3 copy-done.2
  62.7 48.7 %collective-permute-done.1 = bf16[512,2048]{1,0:T(8,128)(2,1)} collective-permute-done((bf16[512,2048]{1,0:T(8,128)(2,1)S(1)}, bf16[512,2048]{1,0:T(8,128)(2,1)}, u32[]{:S(2)}, u32[]{:S(2)}) %collective-permute-start.1) | collective-permute-done | bytes 2097184 | tf_op jit(solution)/shard_map/ppermute | solution.py:30
  111.5 1.0 multiply_cosine_fusion
  112.5 47.0 %collective-permute-done.2 = bf16[512,2048]{1,0:T(8,128)(2,1)} collective-permute-done((bf16[512,2048]{1,0:T(8,128)(2,1)}, bf16[512,2048]{1,0:T(8,128)(2,1)}, u32[]{:S(2)}, u32[]{:S(2)}) %collective-permute-start.2) | collective-permute-done | bytes 2097184 | tf_op jit(solution)/shard_map/ppermute | solution.py:30
  159.5 1.7 constant_dynamic-update-slice_fusion.7
  161.2 1.7 constant_dynamic-update-slice_fusion.6
  163.4 1.7 constant_dynamic-update-slice_fusion.3
  165.2 1.7 constant_dynamic-update-slice_fusion.2
  167.4 5.7 %copy-done.4 = bf16[512,16384]{1,0:T(8,128)(2,1)} copy-done((bf16[512,16384]{1,0:T(8,128)(2,1)}, bf16[512,16384]{1,0:T(8,128)(2,1)S(1)}, u32[]{:S(2)}) %copy-start.4) | copy-done | bytes 16777240
  173.2 1.7 fusion.20
  174.9 19.5 %fusion.28 = f32[512,1536]{1,0:T(8,128)S(1)} fusion(bf16[8192,1536]{1,0:T(8,128)(2,1)} %all-gather.6.cloned.1.call-done, f32[8192]{0:T(1024)S(1)} %copy-done.11, f32[512]{0:T(512)S(1)} %add_rsqrt_fusion, bf16[512,16384]{1,0:T(8,128)(2,1)} %copy-done.4, s32[]{:T(128)S(6)} %select_n.21, f32[1536]{0:T(1024)S(1)} %pad_maximum_fusion.3), kind=kOutput, calls=%fused_computation.36 | convolution fusion | flops 12902465536 | bytes 36741124 | tf_op jit(solution)/shard_map/dot_general | solution.py:41
  194.4 1.6 copy-done.5
  198.1 1.8 copy_bitcast_fusion
  200.5 8.8 %all-gather = s32[8,1,512]{2,1,0:T(1,128)S(1)} all-gather(s32[1,1,512]{2,1,0:T(1,128)S(1)} %bitcast.69), channel_id=1, replica_groups=mesh['seq'=8,'tensor'=4] {'seq'}, dimensions={0}, use_global_device_ids=true | all-gather | bytes 18432 | tf_op jit(solution)/shard_map/all_gather | solution.py:90
  209.4 1.7 slice_bitcast_fusion
  211.6 0.9 subtract_convert_fusion
  212.8 1.5 pad_maximum_fusion.1
  214.3 9.4 %all-gather.8.cloned.1.call-done = bf16[4096,2,128]{2,0,1:T(8,128)(2,1)} async-done(((bf16[512,2,128]{2,0,1:T(8,128)(2,1)}), bf16[4096,2,128]{2,0,1:T(8,128)(2,1)}) %all-gather.8.cloned.1.call-update) | async-done | bytes 2097168 | tf_op jit(solution)/shard_map/all_gather | solution.py:88
  223.7 29.7 %all-gather.10.cloned.1.call-done = bf16[4096,2,128]{2,0,1:T(8,128)(2,1)} async-done(((bf16[512,2,128]{2,0,1:T(8,128)(2,1)}), bf16[4096,2,128]{2,0,1:T(8,128)(2,1)}) %all-gather.10.cloned.1.call-update) | async-done | bytes 2097168 | tf_op jit(solution)/shard_map/all_gather | solution.py:89
  253.4 97.0 %while.15 = (s32[]{:T(128)}, f32[2,4,512]{2,1,0:T(4,128)S(1)}, f32[2,4,512]{2,1,0:T(4,128)S(1)}, f32[2,4,512,128]{3,2,1,0:T(8,128)S(1)}, s32[2,2048]{1,0:T(2,128...) while((s32[]{:T(128)}, f32[2,4,512]{2,1,0:T(4,128)S(1)}, ...), condition=%wide.region_4.5_spmd.clone, body=%wide.region_1.4_spmd.clone.sunk | while | flops 4406661120 | bytes 112487544 | solution.py:102
  254.2 16.7 %fusion.50 = (f32[2,4,512]{2,1,0:T(4,128)S(1)}, f32[2,2048,512,4]{2,1,3,0:T(8,128)}) fusion(pred[512,2048]{0,1:T(8,128)(4,1)S(1)} %broadcast_compare_fusion.2, bf16[512,2,4,128]{3,0,2,1:T(8,128)(2,1)} %get-tuple-element.222, bf16[2,2048,2,128]{3,1,0,2:T(8,128)(2,1)} %get-tuple-element.221, s32[]{:T(128)} %get-tuple-element.204), kind=kOutput, calls=%fused_computation.2.clone.1 | convolution fusion | flops 2172645376 | bytes 36717056 | tf_op jit(solution)/shard_map/while/body/eval_jaxpr/tgcd,sgd->gcts/dot_general | solution.py:66
  270.9 14.9 %fusion.51 = f32[2,4,512]{2,1,0:T(4,128)S(1)} fusion(f32[2,2048,512,4]{2,1,3,0:T(8,128)} %get-tuple-element.190, f32[2,4,512]{2,1,0:T(4,128)S(1)} %select_maximum_fusion.2, pred[512,2048]{0,1:T(8,128)(4,1)S(1)} %broadcast_compare_fusion.2), kind=kLoop, calls=%fused_computation.4.clone.1 | loop fusion | flops 41938944 | bytes 34635776 | tf_op jit(solution)/shard_map/while/body/eval_jaxpr/reduce_sum | solution.py:74
  285.8 17.8 %fusion.53 = f32[2,4,512,128]{3,2,1,0:T(8,128)S(1)} fusion(f32[2,4,512,128]{3,2,1,0:T(8,128)S(1)} %get-tuple-element.207, f32[2,2048,512,4]{2,1,3,0:T(8,128)} %get-tuple-element.190, f32[2,4,512]{2,1,0:T(4,128)S(1)} %select_maximum_fusion.2, pred[512,2048]{0,1:T(8,128)(4,1)S(1)} %broadcast_compare_fusion.2, ...), kind=kOutput, calls=%fused_computation.8.clone.1 | convolution fusion | flops 2190999552 | bytes 39879168 | tf_op jit(solution)/shard_map/while/body/eval_jaxpr/gcts,sgd->gctd/dot_general | solution.py:75
  304.5 15.0 %fusion.50 = (f32[2,4,512]{2,1,0:T(4,128)S(1)}, f32[2,2048,512,4]{2,1,3,0:T(8,128)}) fusion(pred[512,2048]{0,1:T(8,128)(4,1)S(1)} %broadcast_compare_fusion.2, bf16[512,2,4,128]{3,0,2,1:T(8,128)(2,1)} %get-tuple-element.222, bf16[2,2048,2,128]{3,1,0,2:T(8,128)(2,1)} %get-tuple-element.221, s32[]{:T(128)} %get-tuple-element.204), kind=kOutput, calls=%fused_computation.2.clone.1 | convolution fusion | flops 2172645376 | bytes 36717056 | tf_op jit(solution)/shard_map/while/body/eval_jaxpr/tgcd,sgd->gcts/dot_general | solution.py:66
  319.5 15.4 %fusion.51 = f32[2,4,512]{2,1,0:T(4,128)S(1)} fusion(f32[2,2048,512,4]{2,1,3,0:T(8,128)} %get-tuple-element.190, f32[2,4,512]{2,1,0:T(4,128)S(1)} %select_maximum_fusion.2, pred[512,2048]{0,1:T(8,128)(4,1)S(1)} %broadcast_compare_fusion.2), kind=kLoop, calls=%fused_computation.4.clone.1 | loop fusion | flops 41938944 | bytes 34635776 | tf_op jit(solution)/shard_map/while/body/eval_jaxpr/reduce_sum | solution.py:74
  334.9 15.5 %fusion.53 = f32[2,4,512,128]{3,2,1,0:T(8,128)S(1)} fusion(f32[2,4,512,128]{3,2,1,0:T(8,128)S(1)} %get-tuple-element.207, f32[2,2048,512,4]{2,1,3,0:T(8,128)} %get-tuple-element.190, f32[2,4,512]{2,1,0:T(4,128)S(1)} %select_maximum_fusion.2, pred[512,2048]{0,1:T(8,128)(4,1)S(1)} %broadcast_compare_fusion.2, ...), kind=kOutput, calls=%fused_computation.8.clone.1 | convolution fusion | flops 2190999552 | bytes 39879168 | tf_op jit(solution)/shard_map/while/body/eval_jaxpr/gcts,sgd->gctd/dot_general | solution.py:75
  352.8 17.2 %convolution_convert_fusion = bf16[512,8192]{1,0:T(8,128)(2,1)} fusion(bf16[512,1024]{1,0:T(8,128)(2,1)S(1)} %convert_element_type.44, bf16[1024,8192]{1,0:T(8,128)(2,1)} %all-gather.12.cloned.1.call-done), kind=kOutput, calls=%fused_computation.30 | convolution fusion | flops 8594128896 | bytes 26214400 | tf_op jit(solution)/shard_map/dot_general | solution.py:110
  370.0 144.7 %reduce-scatter.2.cloned.1.call-done = bf16[512,2048]{1,0:T(8,128)(2,1)} async-done(((bf16[512,8192]{1,0:T(8,128)(2,1)}), bf16[512,2048]{1,0:T(8,128)(2,1)}) %reduce-scatter.2.cloned.1.call-update) | async-done | bytes 2097168 | tf_op jit(solution)/shard_map/reduce_scatter | solution.py:115
  514.7 3.7 add_convert_fusion
  (69 shorter events, 8.5 us)
Async XLA Ops:
  7.2 3.5 copy-start
  7.2 104.3 %copy-start.7 = (s32[512]{0:T(512)S(1)}, s32[512]{0:T(512)}, u32[]{:S(2)}) copy-start(s32[512]{0:T(512)} %param.13) | copy-start | bytes 6148
  7.2 104.3 %copy-start.8 = (f32[1024]{0:T(1024)S(1)}, f32[1024]{0:T(1024)}, u32[]{:S(2)}) copy-start(f32[1024]{0:T(1024)} %param.18) | copy-start | bytes 12292
  7.2 104.3 %copy-start.10 = (f32[256]{0:T(256)S(1)}, f32[256]{0:T(256)}, u32[]{:S(2)}) copy-start(f32[256]{0:T(256)} %param.19) | copy-start | bytes 3076
  7.2 104.3 %copy-start.9 = (f32[256]{0:T(256)S(1)}, f32[256]{0:T(256)}, u32[]{:S(2)}) copy-start(f32[256]{0:T(256)} %param.20) | copy-start | bytes 3076
  7.2 167.7 %all-gather.6.cloned.1.call-start = ((), (), s32[]{:S(2)}) async-start(), calls=%async_computation.1 | async-start | bytes 28311552 | tf_op jit(solution)/shard_map/all_gather | solution.py:42
  10.6 213.1 %all-gather.8.cloned.1.call-start = ((), (), s32[]{:S(2)}) async-start(), calls=%async_computation.2 | async-start | bytes 2359296 | tf_op jit(solution)/shard_map/all_gather | solution.py:88
  10.6 50.8 %collective-permute-start = (bf16[512,2048]{1,0:T(8,128)(2,1)S(1)}, bf16[512,2048]{1,0:T(8,128)(2,1)S(1)}, u32[]{:S(2)}, u32[]{:S(2)}) collective-permute-start(bf16[512,2048]{1,0:T(8,128)(2,1)S(1)} %copy-done), channel_id=1, source_target_pairs={{0,1},{1,2},{2,3},{3,0},{4,5},{5,6},{6,7},{7,4},{8,9},{9,10},{10,1... | collective-permute-start | bytes 6291464 | tf_op jit(solution)/shard_map/ppermute | solution.py:30
  61.4 1.3 copy-start.2
  62.7 48.7 %collective-permute-start.1 = (bf16[512,2048]{1,0:T(8,128)(2,1)S(1)}, bf16[512,2048]{1,0:T(8,128)(2,1)}, u32[]{:S(2)}, u32[]{:S(2)}) collective-permute-start(bf16[512,2048]{1,0:T(8,128)(2,1)S(1)} %collective-permute-done), channel_id=1, source_target_pairs={{0,1},{1,2},{2,3},{3,0},{4,5},{5,6},{6,7},{7,4},{8,9},{9,10},{10,1... | collective-permute-start | bytes 6291464 | tf_op jit(solution)/shard_map/ppermute | solution.py:30
  111.4 48.1 %collective-permute-start.2 = (bf16[512,2048]{1,0:T(8,128)(2,1)}, bf16[512,2048]{1,0:T(8,128)(2,1)}, u32[]{:S(2)}, u32[]{:S(2)}) collective-permute-start(bf16[512,2048]{1,0:T(8,128)(2,1)} %collective-permute-done.1), channel_id=1, source_target_pairs={{0,1},{1,2},{2,3},{3,0},{4,5},{5,6},{6,7},{7,4},{8,9},{9,10},{10,1... | collective-permute-start | bytes 6291464 | tf_op jit(solution)/shard_map/ppermute | solution.py:30
  111.4 51.5 %copy-start.3 = (bf16[512,2048]{1,0:T(8,128)(2,1)S(1)}, bf16[512,2048]{1,0:T(8,128)(2,1)}, u32[]{:S(2)}) copy-start(bf16[512,2048]{1,0:T(8,128)(2,1)} %copy-done.2) | copy-start | bytes 6291460
  166.9 8.0 %copy-start.11 = (f32[8192]{0:T(1024)S(1)}, f32[8192]{0:T(1024)}, u32[]{:S(2)}) copy-start(f32[8192]{0:T(1024)} %param.14) | copy-start | bytes 98308
  167.4 5.7 %copy-start.4 = (bf16[512,16384]{1,0:T(8,128)(2,1)}, bf16[512,16384]{1,0:T(8,128)(2,1)S(1)}, u32[]{:S(2)}) copy-start(bf16[512,16384]{1,0:T(8,128)(2,1)S(1)} %constant_dynamic-update-slice_fusion) | copy-start | bytes 50331652
  194.4 1.6 copy-start.5
  198.0 55.4 %all-gather.10.cloned.1.call-start = ((), (), s32[]{:S(2)}) async-start(), calls=%async_computation.3 | async-start | bytes 2359296 | tf_op jit(solution)/shard_map/all_gather | solution.py:89
  199.8 152.9 %all-gather.12.cloned.1.call-start = ((), (), s32[]{:S(2)}) async-start(), calls=%async_computation.4 | async-start | bytes 18874368 | tf_op jit(solution)/shard_map/all_gather | solution.py:112
  200.4 314.3 %reduce-scatter.2.cloned.1.call-start = ((), (), s32[]{:S(2)}) async-start(), calls=%async_computation.5 | async-start | bytes 10485760 | tf_op jit(solution)/shard_map/reduce_scatter | solution.py:115
  352.7 17.2 %copy-start.6 = (bf16[512,1024]{1,0:T(8,128)(2,1)}, bf16[512,1024]{1,0:T(8,128)(2,1)S(1)}, u32[]{:S(2)}) copy-start(bf16[512,1024]{1,0:T(8,128)(2,1)S(1)} %convert_element_type.44) | copy-start | bytes 3145732
  370.0 144.7 %copy-start.1 = (bf16[512,2048]{1,0:T(8,128)(2,1)S(1)}, bf16[512,2048]{1,0:T(8,128)(2,1)}, u32[]{:S(2)}) copy-start(bf16[512,2048]{1,0:T(8,128)(2,1)} %param.12) | copy-start | bytes 6291460
Sparse Core Ops, SparseCore 0:
  10.7 127.9 all-gather.5
  198.1 25.5 all-gather.7
  225.6 27.7 all-gather.9
  255.2 89.7 all-gather.11
  370.1 144.5 reduce-scatter.1
